TPU v7x, 32 devices: a whole 2x2x4 slice. The times are simulated.
32 devices in a mesh: tm: 8 (over z, core), block: 4 (over y, x).
Axes of the slice: x: 2, y: 2, z: 4, core: 2. Of those that a mesh axis runs over, the one named last changes fastest.
Arguments:
- state: float32 [16, 4, 256, 512], P('tm', None, None, 'block'), may hold values from -6 to 6
- far_field: float32 [16, 4, 512], P('tm', None, 'block'), may hold values from -6 to 6
- face_index: int32 [16, 512], P('tm', 'block'), may hold values from 0 to 255, as said below
- face_weight: float32 [16, 4, 512], P('tm', None, 'block'), may hold values from 0.05 to 0.45
- mean_flow: float32 [2, 2], replicated, may hold values from -0.6 to 0.6
Outputs:
- new_state: float32 [16, 4, 256, 512], P('tm', None, None, 'block')
Inputs may be any that keep to these rules, and one draw needn't show every extreme that they name: `face_index`: each face's index points into the opposite row's 2 * 128 interface faces laid end to end; the 4 faces read wrap around that cycle. At each level, the faces of one blade row take distinct first indices, every face of the opposite row exactly once.
All inputs are finite; a program needn't handle non-finite values.
Results may differ from a plain program's by a relative error of at most 0.00016.
Values sent between devices are 32-bit elements; how exact they have to be, the bound alone decides.
A program may use at most 64 MiB of HBM per device.

v0:
```python
import jax
import jax.numpy as jnp
from jax import lax
from jax.sharding import PartitionSpec as P

SECTION_FACTORS = (0.075, 0.05, 0.1125, 0.15, 0.3)
OMEGA = 1.0
DISSIPATION = 0.2


def derivative_matrix(count):
    index = jnp.arange(count)
    offsets = index[:, None] - index[None, :]
    angle = jnp.pi * offsets.astype(jnp.float32) / count
    parity_sign = 1.0 - 2.0 * (offsets % 2).astype(jnp.float32)
    safe_angle = jnp.where(offsets == 0, 0.5 * jnp.pi, angle)
    cotangent = jnp.cos(safe_angle) / jnp.sin(safe_angle)
    return jnp.where(offsets == 0, 0.0, 0.5 * parity_sign * cotangent)


def interface_ghost(faces, table, weight, row_side, width):
    level_count = faces.shape[0]
    cycle_size = faces.shape[2] // 2
    grid = faces.reshape(level_count, 4, 2, cycle_size)
    other = jnp.take(grid, 1 - row_side, axis=2)
    shape = (level_count, 4, width)
    total = jnp.zeros(shape, jnp.float32)
    for offset in range(weight.shape[1]):
        source = (table + offset) % cycle_size
        picked = jnp.take_along_axis(other, jnp.broadcast_to(source[:, None, :], shape), axis=2)
        total = total + weight[:, offset][:, None, :] * picked
    return total


def pitch_neighbours(last_all, first_all):
    half_count = lax.axis_size("block") // 2
    place = lax.axis_index("block")
    row_start = place // half_count * half_count
    in_row = place % half_count
    lower_place = row_start + (in_row + half_count - 1) % half_count
    upper_place = row_start + (in_row + 1) % half_count
    lower_col = lax.dynamic_slice_in_dim(last_all, lower_place, 1, 3)
    upper_col = lax.dynamic_slice_in_dim(first_all, upper_place, 1, 3)
    return (lower_col, upper_col)


def residual(field, lower_ghost, upper_ghost, lower_col, upper_col, speeds):
    speed_u = speeds[0]
    speed_v = speeds[1]
    padded_i = jnp.concatenate([lower_ghost[:, :, None], field, upper_ghost[:, :, None]], axis=2)
    padded_j = jnp.concatenate([lower_col, field, upper_col], axis=3)
    diff_i = padded_i[:, :, 2:] - padded_i[:, :, :-2]
    diff_j = padded_j[..., 2:] - padded_j[..., :-2]
    laplace = (
        padded_i[:, :, 2:]
        - 2.0 * field
        + padded_i[:, :, :-2]
        + (padded_j[..., 2:] - 2.0 * field + padded_j[..., :-2])
    )
    flux_i = jnp.stack(
        [
            speed_u * diff_i[:, 0] + diff_i[:, 1],
            speed_u * diff_i[:, 1] + diff_i[:, 3],
            speed_u * diff_i[:, 2],
            speed_u * diff_i[:, 3] + diff_i[:, 1],
        ],
        axis=1,
    )
    flux_j = jnp.stack(
        [
            speed_v * diff_j[:, 0] + diff_j[:, 2],
            speed_v * diff_j[:, 1],
            speed_v * diff_j[:, 2] + diff_j[:, 3],
            speed_v * diff_j[:, 3] + diff_j[:, 2],
        ],
        axis=1,
    )
    return 0.5 * (flux_i + flux_j) - DISSIPATION * laplace


def shards(state, far_field, face_index, face_weight, mean_flow):
    tm_count = lax.axis_size("tm")
    row_side = lax.axis_index("block") // (lax.axis_size("block") // 2)
    level_here = state.shape[0]
    row_count = state.shape[2]
    width = state.shape[3]
    spectral = derivative_matrix(level_here * tm_count)
    speeds = jnp.take(mean_flow, row_side, axis=0)
    field = state
    for factor in SECTION_FACTORS:
        sent = jnp.where(row_side == 0, field[:, :, row_count - 1], field[:, :, 0])
        face_gathered, last_all, first_all = (
            lax.all_gather(sent[:, :, None, :], "block", axis=3, tiled=True),
            lax.all_gather(field[..., -1:], "block", axis=3, tiled=True),
            lax.all_gather(field[..., :1], "block", axis=3, tiled=True),
        )
        faces = face_gathered.reshape(level_here, 4, -1)
        lower_col, upper_col = pitch_neighbours(last_all, first_all)
        ghost = interface_ghost(faces, face_index, face_weight, row_side, width)
        lower_ghost = jnp.where(row_side == 0, far_field, ghost)
        upper_ghost = jnp.where(row_side == 0, ghost, far_field)
        flux = residual(field, lower_ghost, upper_ghost, lower_col, upper_col, speeds)
        applied = jnp.einsum(
            "nm,mvij->nvij",
            spectral,
            lax.all_to_all(field, "tm", split_axis=2, concat_axis=0, tiled=True),
            precision=lax.Precision.HIGHEST,
        )
        deriv = lax.all_to_all(applied, "tm", split_axis=0, concat_axis=2, tiled=True)
        field = state - factor * (flux + OMEGA * deriv)
    return field


def solution(mesh):
    in_specs = (
        P("tm", None, None, "block"),
        P("tm", None, "block"),
        P("tm", "block"),
        P("tm", None, "block"),
        P(),
    )
    out_specs = P("tm", None, None, "block")
    return jax.shard_map(shards, mesh=mesh, in_specs=in_specs, out_specs=out_specs, check_vma=False)
```

profile of v0, /device:TPU:0, one launch (start us, length us, event | category | flops | bytes accessed | tf_op | source)
XLA Modules:
  0.0 563.2 jit_solution(4083573060886229254)
XLA Ops:
  9.4 8.1 %all_gather.45 = f32[2,4,1,512]{3,2,1,0:T(1,128)S(1)} all-gather(f32[2,4,1,128]{3,2,1,0:T(1,128)S(1)} %broadcast_select_fusion.4), channel_id=1, replica_groups=mesh['tm'=8,'block'=4] {'block'}, dimensions={3}, use_global_device_ids=true | all-gather | bytes 20480 | tf_op jit(solution)/shard_map/all_gather | solution.py:93
  19.7 16.3 %all-to-all-done = f32[2,4,256,128]{3,1,0,2:T(4,128)S(1)} async-done(((f32[2,4,256,128]{3,1,0,2:T(4,128)}), f32[2,4,256,128]{3,1,0,2:T(4,128)S(1)}, u32[]{:S(2)}, u32[]{:S(2)}) %all-to-all-start) | async-done | bytes 1048608 | tf_op jit(solution)/shard_map/all_to_all | solution.py:106
  43.2 10.5 %gather_fusion.3 = f32[1024]{0:T(1024)S(1)} fusion(f32[2,4,256]{2,1,0:T(4,128)S(1)} %fusion.57, s32[1024]{0:T(1024)S(1)} %bitcast.197), kind=kCustom, calls=%fused_computation.3.clone | custom fusion | bytes 20480 | tf_op jit(solution)/shard_map/jit(take_along_axis)/gather | solution.py:30
  53.7 10.5 %gather_fusion.2 = f32[1024]{0:T(1024)S(1)} fusion(f32[2,4,256]{2,1,0:T(4,128)S(1)} %fusion.57, s32[1024]{0:T(1024)S(1)} %bitcast.192), kind=kCustom, calls=%fused_computation.2.clone | custom fusion | bytes 20480 | tf_op jit(solution)/shard_map/jit(take_along_axis)/gather | solution.py:30
  64.2 10.5 %gather_fusion.1 = f32[1024]{0:T(1024)S(1)} fusion(f32[2,4,256]{2,1,0:T(4,128)S(1)} %fusion.57, s32[1024]{0:T(1024)S(1)} %bitcast.207), kind=kCustom, calls=%fused_computation.1.clone | custom fusion | bytes 20480 | tf_op jit(solution)/shard_map/jit(take_along_axis)/gather | solution.py:30
  74.6 10.5 %gather_fusion = f32[1024]{0:T(1024)S(1)} fusion(f32[2,4,256]{2,1,0:T(4,128)S(1)} %fusion.57, s32[1024]{0:T(1024)S(1)} %bitcast.202), kind=kCustom, calls=%fused_computation.clone | custom fusion | bytes 20480 | tf_op jit(solution)/shard_map/jit(take_along_axis)/gather | solution.py:30
  85.8 8.2 %all_gather.47 = f32[2,4,256,4]{2,1,0,3:T(4,128)S(1)} all-gather(f32[2,4,256,1]{2,1,0,3:T(4,128)S(1)} %copy.230), channel_id=1, replica_groups=mesh['tm'=8,'block'=4] {'block'}, dimensions={3}, use_global_device_ids=true | all-gather | bytes 40960 | tf_op jit(solution)/shard_map/all_gather | solution.py:94
  94.4 8.2 %all_gather.46 = f32[2,4,256,4]{2,1,0,3:T(4,128)S(1)} all-gather(f32[2,4,256,1]{2,1,0,3:T(4,128)S(1)} %copy.228), channel_id=1, replica_groups=mesh['tm'=8,'block'=4] {'block'}, dimensions={3}, use_global_device_ids=true | all-gather | bytes 40960 | tf_op jit(solution)/shard_map/all_gather | solution.py:95
  126.6 19.2 %all-to-all-done.2 = f32[2,4,256,128]{3,1,0,2:T(4,128)S(1)} async-done(((f32[2,4,256,128]{3,1,0,2:T(4,128)}), f32[2,4,256,128]{3,1,0,2:T(4,128)S(1)}, u32[]{:S(2)}, u32[]{:S(2)}) %all-to-all-start.2) | async-done | bytes 1048608 | tf_op jit(solution)/shard_map/all_to_all | solution.py:106
  153.0 10.5 %gather_fusion.7 = f32[1024]{0:T(1024)S(1)} fusion(f32[2,4,256]{2,1,0:T(4,128)S(1)} %fusion.56, s32[1024]{0:T(1024)S(1)} %bitcast.198), kind=kCustom, calls=%fused_computation.7.clone | custom fusion | bytes 20480 | tf_op jit(solution)/shard_map/jit(take_along_axis)/gather | solution.py:30
  163.5 10.5 %gather_fusion.6 = f32[1024]{0:T(1024)S(1)} fusion(f32[2,4,256]{2,1,0:T(4,128)S(1)} %fusion.56, s32[1024]{0:T(1024)S(1)} %bitcast.193), kind=kCustom, calls=%fused_computation.6.clone | custom fusion | bytes 20480 | tf_op jit(solution)/shard_map/jit(take_along_axis)/gather | solution.py:30
  173.9 10.5 %gather_fusion.5 = f32[1024]{0:T(1024)S(1)} fusion(f32[2,4,256]{2,1,0:T(4,128)S(1)} %fusion.56, s32[1024]{0:T(1024)S(1)} %bitcast.208), kind=kCustom, calls=%fused_computation.5.clone | custom fusion | bytes 20480 | tf_op jit(solution)/shard_map/jit(take_along_axis)/gather | solution.py:30
  184.4 10.5 %gather_fusion.4 = f32[1024]{0:T(1024)S(1)} fusion(f32[2,4,256]{2,1,0:T(4,128)S(1)} %fusion.56, s32[1024]{0:T(1024)S(1)} %bitcast.203), kind=kCustom, calls=%fused_computation.4.clone | custom fusion | bytes 20480 | tf_op jit(solution)/shard_map/jit(take_along_axis)/gather | solution.py:30
  205.7 8.2 %all_gather.49 = f32[2,4,256,4]{2,1,0,3:T(4,128)S(1)} all-gather(f32[2,4,256,1]{2,1,0,3:T(4,128)S(1)} %copy.185), channel_id=1, replica_groups=mesh['tm'=8,'block'=4] {'block'}, dimensions={3}, use_global_device_ids=true | all-gather | bytes 40960 | tf_op jit(solution)/shard_map/all_gather | solution.py:95
  238.6 19.4 %all-to-all-done.4 = f32[2,4,256,128]{3,1,0,2:T(4,128)S(1)} async-done(((f32[2,4,256,128]{3,1,0,2:T(4,128)}), f32[2,4,256,128]{3,1,0,2:T(4,128)S(1)}, u32[]{:S(2)}, u32[]{:S(2)}) %all-to-all-start.4) | async-done | bytes 1048608 | tf_op jit(solution)/shard_map/all_to_all | solution.py:106
  265.4 10.5 %gather_fusion.11 = f32[1024]{0:T(1024)S(1)} fusion(f32[2,4,256]{2,1,0:T(4,128)S(1)} %fusion.55, s32[1024]{0:T(1024)S(1)} %bitcast.199), kind=kCustom, calls=%fused_computation.11.clone | custom fusion | bytes 20480 | tf_op jit(solution)/shard_map/jit(take_along_axis)/gather | solution.py:30
  275.9 10.5 %gather_fusion.10 = f32[1024]{0:T(1024)S(1)} fusion(f32[2,4,256]{2,1,0:T(4,128)S(1)} %fusion.55, s32[1024]{0:T(1024)S(1)} %bitcast.194), kind=kCustom, calls=%fused_computation.10.clone | custom fusion | bytes 20480 | tf_op jit(solution)/shard_map/jit(take_along_axis)/gather | solution.py:30
  286.3 10.5 %gather_fusion.9 = f32[1024]{0:T(1024)S(1)} fusion(f32[2,4,256]{2,1,0:T(4,128)S(1)} %fusion.55, s32[1024]{0:T(1024)S(1)} %bitcast.209), kind=kCustom, calls=%fused_computation.9.clone | custom fusion | bytes 20480 | tf_op jit(solution)/shard_map/jit(take_along_axis)/gather | solution.py:30
  296.8 10.5 %gather_fusion.8 = f32[1024]{0:T(1024)S(1)} fusion(f32[2,4,256]{2,1,0:T(4,128)S(1)} %fusion.55, s32[1024]{0:T(1024)S(1)} %bitcast.204), kind=kCustom, calls=%fused_computation.8.clone | custom fusion | bytes 20480 | tf_op jit(solution)/shard_map/jit(take_along_axis)/gather | solution.py:30
  318.1 8.2 %all_gather.52 = f32[2,4,256,4]{2,1,0,3:T(4,128)S(1)} all-gather(f32[2,4,256,1]{2,1,0,3:T(4,128)S(1)} %copy.196), channel_id=1, replica_groups=mesh['tm'=8,'block'=4] {'block'}, dimensions={3}, use_global_device_ids=true | all-gather | bytes 40960 | tf_op jit(solution)/shard_map/all_gather | solution.py:95
  351.1 19.4 %all-to-all-done.6 = f32[2,4,256,128]{3,1,0,2:T(4,128)S(1)} async-done(((f32[2,4,256,128]{3,1,0,2:T(4,128)}), f32[2,4,256,128]{3,1,0,2:T(4,128)S(1)}, u32[]{:S(2)}, u32[]{:S(2)}) %all-to-all-start.6) | async-done | bytes 1048608 | tf_op jit(solution)/shard_map/all_to_all | solution.py:106
  378.1 10.5 %gather_fusion.15 = f32[1024]{0:T(1024)S(1)} fusion(f32[2,4,256]{2,1,0:T(4,128)S(1)} %fusion.54, s32[1024]{0:T(1024)S(1)} %bitcast.200), kind=kCustom, calls=%fused_computation.15.clone | custom fusion | bytes 20480 | tf_op jit(solution)/shard_map/jit(take_along_axis)/gather | solution.py:30
  388.6 10.5 %gather_fusion.14 = f32[1024]{0:T(1024)S(1)} fusion(f32[2,4,256]{2,1,0:T(4,128)S(1)} %fusion.54, s32[1024]{0:T(1024)S(1)} %bitcast.195), kind=kCustom, calls=%fused_computation.14.clone | custom fusion | bytes 20480 | tf_op jit(solution)/shard_map/jit(take_along_axis)/gather | solution.py:30
  399.0 10.5 %gather_fusion.13 = f32[1024]{0:T(1024)S(1)} fusion(f32[2,4,256]{2,1,0:T(4,128)S(1)} %fusion.54, s32[1024]{0:T(1024)S(1)} %bitcast.210), kind=kCustom, calls=%fused_computation.13.clone | custom fusion | bytes 20480 | tf_op jit(solution)/shard_map/jit(take_along_axis)/gather | solution.py:30
  409.5 10.5 %gather_fusion.12 = f32[1024]{0:T(1024)S(1)} fusion(f32[2,4,256]{2,1,0:T(4,128)S(1)} %fusion.54, s32[1024]{0:T(1024)S(1)} %bitcast.205), kind=kCustom, calls=%fused_computation.12.clone | custom fusion | bytes 20480 | tf_op jit(solution)/shard_map/jit(take_along_axis)/gather | solution.py:30
  430.8 8.2 %all_gather.55 = f32[2,4,256,4]{2,1,0,3:T(4,128)S(1)} all-gather(f32[2,4,256,1]{2,1,0,3:T(4,128)S(1)} %copy.207), channel_id=1, replica_groups=mesh['tm'=8,'block'=4] {'block'}, dimensions={3}, use_global_device_ids=true | all-gather | bytes 40960 | tf_op jit(solution)/shard_map/all_gather | solution.py:95
  463.8 19.4 %all-to-all-done.8 = f32[2,4,256,128]{3,1,0,2:T(4,128)S(1)} async-done(((f32[2,4,256,128]{3,1,0,2:T(4,128)}), f32[2,4,256,128]{3,1,0,2:T(4,128)S(1)}, u32[]{:S(2)}, u32[]{:S(2)}) %all-to-all-start.8) | async-done | bytes 1048608 | tf_op jit(solution)/shard_map/all_to_all | solution.py:106
  490.5 10.5 %gather_fusion.19 = f32[1024]{0:T(1024)S(1)} fusion(f32[2,4,256]{2,1,0:T(4,128)S(1)} %fusion.53, s32[1024]{0:T(1024)S(1)} %bitcast.201), kind=kCustom, calls=%fused_computation.19.clone | custom fusion | bytes 20480 | tf_op jit(solution)/shard_map/jit(take_along_axis)/gather | solution.py:30
  501.0 10.5 %gather_fusion.18 = f32[1024]{0:T(1024)S(1)} fusion(f32[2,4,256]{2,1,0:T(4,128)S(1)} %fusion.53, s32[1024]{0:T(1024)S(1)} %bitcast.196), kind=kCustom, calls=%fused_computation.18.clone | custom fusion | bytes 20480 | tf_op jit(solution)/shard_map/jit(take_along_axis)/gather | solution.py:30
  511.5 10.5 %gather_fusion.17 = f32[1024]{0:T(1024)S(1)} fusion(f32[2,4,256]{2,1,0:T(4,128)S(1)} %fusion.53, s32[1024]{0:T(1024)S(1)} %bitcast.211), kind=kCustom, calls=%fused_computation.17.clone | custom fusion | bytes 20480 | tf_op jit(solution)/shard_map/jit(take_along_axis)/gather | solution.py:30
  522.0 10.5 %gather_fusion.16 = f32[1024]{0:T(1024)S(1)} fusion(f32[2,4,256]{2,1,0:T(4,128)S(1)} %fusion.53, s32[1024]{0:T(1024)S(1)} %bitcast.206), kind=kCustom, calls=%fused_computation.16.clone | custom fusion | bytes 20480 | tf_op jit(solution)/shard_map/jit(take_along_axis)/gather | solution.py:30
  543.2 8.2 %all_gather.58 = f32[2,4,256,4]{2,1,0,3:T(4,128)S(1)} all-gather(f32[2,4,256,1]{2,1,0,3:T(4,128)S(1)} %copy.218), channel_id=1, replica_groups=mesh['tm'=8,'block'=4] {'block'}, dimensions={3}, use_global_device_ids=true | all-gather | bytes 40960 | tf_op jit(solution)/shard_map/all_gather | solution.py:95
  (200 shorter events, 202.2 us)
Async XLA Ops:
  2.9 6.5 %copy-start = (f32[2,4,256,128]{3,2,1,0:T(8,128)S(1)}, f32[2,4,256,128]{3,2,1,0:T(8,128)}, u32[]{:S(2)}) copy-start(f32[2,4,256,128]{3,2,1,0:T(8,128)} %param.9) | copy-start | bytes 3145732
  2.9 33.0 %all-to-all-start = ((f32[2,4,256,128]{3,1,0,2:T(4,128)}), f32[2,4,256,128]{3,1,0,2:T(4,128)S(1)}, u32[]{:S(2)}, u32[]{:S(2)}) async-start(f32[2,4,256,128]{3,1,0,2:T(4,128)} %copy.178), calls=%async_computation | async-start | bytes 2097152 | tf_op jit(solution)/shard_map/all_to_all | solution.py:106
  38.9 69.8 %all-to-all-start.1 = ((f32[16,4,32,128]{3,2,1,0:T(8,128)}), f32[16,4,32,128]{3,2,1,0:T(8,128)}, u32[]{:S(2)}, u32[]{:S(2)}) async-start(f32[16,4,32,128]{3,2,1,0:T(8,128)} %copy.180), calls=%async_computation.1 | async-start | bytes 2097152 | tf_op jit(solution)/shard_map/all_to_all | solution.py:109
  74.6 10.5 %copy-start.13 = (f32[2,4,256,1]{3,2,1,0:T(8,128)S(1)}, f32[2,4,256,1]{3,2,1,0:T(8,128)}, u32[]{:S(2)}) copy-start(f32[2,4,256,1]{3,2,1,0:T(8,128)} %get-tuple-element.105) | copy-start | bytes 24580
  102.9 2.7 copy-start.11
  108.7 1.5 copy-start.12
  108.7 1.6 copy-start.17
  108.8 1.7 copy-start.18
  108.8 1.7 copy-start.19
  108.8 1.8 copy-start.21
  114.2 31.6 %all-to-all-start.2 = ((f32[2,4,256,128]{3,1,0,2:T(4,128)}), f32[2,4,256,128]{3,1,0,2:T(4,128)S(1)}, u32[]{:S(2)}, u32[]{:S(2)}) async-start(f32[2,4,256,128]{3,1,0,2:T(4,128)} %copy.189), calls=%async_computation.2 | async-start | bytes 2097152 | tf_op jit(solution)/shard_map/all_to_all | solution.py:106
  148.7 71.9 %all-to-all-start.3 = ((f32[16,4,32,128]{3,2,1,0:T(8,128)}), f32[16,4,32,128]{3,2,1,0:T(8,128)}, u32[]{:S(2)}, u32[]{:S(2)}) async-start(f32[16,4,32,128]{3,2,1,0:T(8,128)} %copy.191), calls=%async_computation.3 | async-start | bytes 2097152 | tf_op jit(solution)/shard_map/all_to_all | solution.py:109
  205.7 11.8 %copy-start.4 = (f32[2,4,256,1]{3,2,1,0:T(8,128)}, f32[2,4,256,1]{3,2,1,0:T(8,128)S(1)}, u32[]{:S(2)}) copy-start(f32[2,4,256,1]{3,2,1,0:T(8,128)S(1)} %copy.234) | copy-start | bytes 24580
  220.6 1.5 copy-start.5
  220.6 1.9 copy-start.8
  226.5 31.6 %all-to-all-start.4 = ((f32[2,4,256,128]{3,1,0,2:T(4,128)}), f32[2,4,256,128]{3,1,0,2:T(4,128)S(1)}, u32[]{:S(2)}, u32[]{:S(2)}) async-start(f32[2,4,256,128]{3,1,0,2:T(4,128)} %copy.200), calls=%async_computation.4 | async-start | bytes 2097152 | tf_op jit(solution)/shard_map/all_to_all | solution.py:106
  260.9 72.1 %all-to-all-start.5 = ((f32[16,4,32,128]{3,2,1,0:T(8,128)}), f32[16,4,32,128]{3,2,1,0:T(8,128)}, u32[]{:S(2)}, u32[]{:S(2)}) async-start(f32[16,4,32,128]{3,2,1,0:T(8,128)} %copy.202), calls=%async_computation.5 | async-start | bytes 2097152 | tf_op jit(solution)/shard_map/all_to_all | solution.py:109
  318.1 11.8 %copy-start.6 = (f32[2,4,256,1]{3,2,1,0:T(8,128)}, f32[2,4,256,1]{3,2,1,0:T(8,128)S(1)}, u32[]{:S(2)}) copy-start(f32[2,4,256,1]{3,2,1,0:T(8,128)S(1)} %copy.237) | copy-start | bytes 24580
  333.0 1.5 copy-start.7
  333.0 1.9 copy-start.9
  337.2 103.1 %copy-start.1 = (f32[2,4,256,128]{3,2,1,0:T(8,128)}, f32[2,4,256,128]{3,2,1,0:T(8,128)S(1)}, u32[]{:S(2)}) copy-start(f32[2,4,256,128]{3,2,1,0:T(8,128)S(1)} %fusion.14) | copy-start | bytes 3145732
  338.9 31.6 %all-to-all-start.6 = ((f32[2,4,256,128]{3,1,0,2:T(4,128)}), f32[2,4,256,128]{3,1,0,2:T(4,128)S(1)}, u32[]{:S(2)}, u32[]{:S(2)}) async-start(f32[2,4,256,128]{3,1,0,2:T(4,128)} %copy.211), calls=%async_computation.6 | async-start | bytes 2097152 | tf_op jit(solution)/shard_map/all_to_all | solution.py:106
  373.4 72.3 %all-to-all-start.7 = ((f32[16,4,32,128]{3,2,1,0:T(8,128)}), f32[16,4,32,128]{3,2,1,0:T(8,128)}, u32[]{:S(2)}, u32[]{:S(2)}) async-start(f32[16,4,32,128]{3,2,1,0:T(8,128)} %copy.213), calls=%async_computation.7 | async-start | bytes 2097152 | tf_op jit(solution)/shard_map/all_to_all | solution.py:109
  445.7 1.5 copy-start.2
  445.7 1.9 copy-start.10
  451.6 31.6 %all-to-all-start.8 = ((f32[2,4,256,128]{3,1,0,2:T(4,128)}), f32[2,4,256,128]{3,1,0,2:T(4,128)S(1)}, u32[]{:S(2)}, u32[]{:S(2)}) async-start(f32[2,4,256,128]{3,1,0,2:T(4,128)} %copy.222), calls=%async_computation.8 | async-start | bytes 2097152 | tf_op jit(solution)/shard_map/all_to_all | solution.py:106
  486.1 72.1 %all-to-all-start.9 = ((f32[16,4,32,128]{3,2,1,0:T(8,128)}), f32[16,4,32,128]{3,2,1,0:T(8,128)}, u32[]{:S(2)}, u32[]{:S(2)}) async-start(f32[16,4,32,128]{3,2,1,0:T(8,128)} %copy.224), calls=%async_computation.9 | async-start | bytes 2097152 | tf_op jit(solution)/shard_map/all_to_all | solution.py:109
  558.2 1.5 copy-start.3
  558.2 1.6 copy-start.14
  558.2 1.7 copy-start.15
  558.2 1.7 copy-start.16
  558.2 1.8 copy-start.20
  (4 other events, 3.0 us)
where the time goes:
time: 572 us; the launch traced here: 563 us
  local copies, waits for them, and re-layouts  262 us (46%)
  blocking collectives  114 us (20%)
  waiting for transfers between devices  93.6 us (16%)
  starting transfers between devices  48.6 us (8%)
  other arithmetic  38.1 us (7%)
    gather x20, local copies, waits for them, and re-layouts, interface_ghost(): jnp.take_along_axis(other, jnp.broadcast_to(source[:, None, :], shape), a...  209 us
    all_to_all x5, waiting for transfers between devices, shards(): lax.all_to_all(field, 'tm', split_axis=2, concat_axis=0, tiled=True)  93.6 us
    all_gather x5, blocking collectives, shards(): lax.all_gather(field[..., :1], 'block', axis=3, tiled=True)  40.8 us
    all_gather x5, blocking collectives, shards(): lax.all_gather(field[..., -1:], 'block', axis=3, tiled=True)  37 us
    all_gather x5, blocking collectives, shards(): lax.all_gather(sent[:, :, None, :], 'block', axis=3, tiled=True)  36.6 us
    all_to_all x5, starting transfers between devices, shards(): lax.all_to_all(field, 'tm', split_axis=2, concat_axis=0, tiled=True)  26.6 us
    all_to_all x5, starting transfers between devices, shards(): lax.all_to_all(applied, 'tm', split_axis=0, concat_axis=2, tiled=True)  22 us
    unnamed x65, local copies, waits for them, and re-layouts  14.8 us
  transfers between devices with their start and end apart: 10, of which 5 were waited for; matrix products, arithmetic and copies ran while one was open for 46% of the time, Pallas kernels for 0%

commit v1 on v0

v1 whole, which is shorter than its diff:
```python
import functools
import math

import jax
import jax.numpy as jnp
from jax import lax
from jax.experimental import pallas as pl
from jax.experimental.pallas import tpu as pltpu
from jax.sharding import PartitionSpec as P

SECTION_FACTORS = (0.075, 0.05, 0.1125, 0.15, 0.3)
OMEGA = 1.0
DISSIPATION = 0.2
PAD = 8
MESH = pl.DeviceIdType.MESH


def split_coefficients(count):
    half = count // 2
    d = [0.0] + [0.5 * (-1) ** k / math.tan(math.pi * k / count) for k in range(1, half)] + [0.0]
    even = [0.5 * OMEGA * (d[m] - d[half - m]) for m in range(half)]
    odd = [0.5 * OMEGA * (d[m] + d[half - m]) for m in range(half)]
    even[0] = odd[0] = 0.0
    return even, odd


def time_term(q, even, odd):
    half = len(q) // 2
    quarter = half // 2
    e = [q[n] + q[n + half] for n in range(half)]
    o = [q[n] - q[n + half] for n in range(half)]

    def odd_at(n):
        return (o[n % half], -1.0 if (n // half) % 2 else 1.0)

    low, high = [], []
    for n in range(half):
        ev = None
        od = None
        for m in range(1, quarter):
            term = even[m] * (e[(n - m) % half] - e[(n + m) % half])
            ev = term if ev is None else ev + term
            (a, sa), (b, sb) = odd_at(n - m), odd_at(n + m)
            pair = a - b if sa == sb else a + b
            term = (odd[m] * sa) * pair
            od = term if od is None else od + term
        a, sa = odd_at(n - quarter)
        od = od + (odd[quarter] * sa) * a
        low.append(ev + od)
        high.append(ev - od)
    return low + high


def kernel(dims, state, far, fidx, fw, mf, out, x0, qa, qb, ef, el, rl, ru, cs, cl, cu,
           face, ff, wts, fi, lane_ix, blk_ix, ww, gh,
           in_s, in_r, out_s, out_r, p_s, p_r, h_s, h_r, f_s, f_r, loc):
    tm_n, half, L, R, K = dims
    NT = tm_n * L
    cycle = half * 128
    tiles = R // 8
    nsec = len(SECTION_FACTORS)
    me = lax.axis_index("tm")
    blk = lax.axis_index("block")
    side = lax.div(blk, half)
    place = lax.rem(blk, half)
    row0 = side * half
    lower_b = row0 + lax.rem(place + half - 1, half)
    upper_b = row0 + lax.rem(place + 1, half)
    other0 = (1 - side) * half
    step = 1 - 2 * side
    is_last = me == tm_n - 1
    is_far = me == 0
    rchunk = side * (tm_n - 1) + step * me
    has_lower = rchunk > 0
    has_upper = rchunk < tm_n - 1
    ghost_row = jnp.where(side == 0, PAD + R, PAD - 1)
    far_row = jnp.where(side == 0, PAD - 1, PAD + R)

    def rc(src, dst, ss, rs, dev):
        return pltpu.make_async_remote_copy(src_ref=src, dst_ref=dst, send_sem=ss, recv_sem=rs,
                                            device_id=dev, device_id_type=MESH)

    def rows(p):
        return pl.ds(pl.multiple_of((side * (tm_n - 1) + step * p) * R, R), R)

    def lev(p):
        return pl.ds(p * L, L)

    def peer(t):
        return lax.rem(me + t, tm_n)

    bar = pltpu.get_barrier_semaphore()

    @pl.loop(1, tm_n)
    def _(t):
        pl.semaphore_signal(bar, inc=1, device_id={"tm": peer(t)}, device_id_type=MESH)

    pl.semaphore_signal(bar, inc=1, device_id={"block": lower_b}, device_id_type=MESH)
    pl.semaphore_signal(bar, inc=1, device_id={"block": upper_b}, device_id_type=MESH)

    @pl.when(is_last)
    def _():
        for h in range(half):
            pl.semaphore_signal(bar, inc=1, device_id={"block": other0 + h}, device_id_type=MESH)

    own = pltpu.make_async_copy(state.at[:, :, rows(me)], x0.at[lev(me)], loc.at[0])
    own.start()
    pl.semaphore_wait(bar, tm_n + 1 + jnp.where(is_last, half, 0))

    def in_copy(p, src_tm):
        return rc(state.at[:, :, rows(p)], x0.at[lev(src_tm)], in_s.at[p], in_r.at[src_tm], {"tm": p})

    @pl.loop(1, tm_n)
    def _(t):
        p = peer(t)
        in_copy(p, me).start()

    def far_copy(src_tm):
        return rc(far, ff.at[lev(src_tm)], p_s.at[0], p_r.at[0, src_tm], {"tm": 0})

    def wt_copy(src_tm):
        return rc(fw, wts.at[lev(src_tm)], p_s.at[1], p_r.at[1, src_tm], {"tm": tm_n - 1})

    def ix_copy(src_tm):
        return rc(fidx, fi.at[src_tm], p_s.at[2], p_r.at[2, src_tm], {"tm": tm_n - 1})

    own_far = pltpu.make_async_copy(far, ff.at[lev(me)], loc.at[1])
    own_wt = pltpu.make_async_copy(fw, wts.at[lev(me)], loc.at[2])
    own_ix = pltpu.make_async_copy(fidx, fi.at[me], loc.at[3])

    @pl.when(is_far)
    def _():
        own_far.start()

    @pl.when(jnp.logical_not(is_far))
    def _():
        far_copy(me).start()

    @pl.when(is_last)
    def _():
        own_wt.start()
        own_ix.start()

    @pl.when(jnp.logical_not(is_last))
    def _():
        wt_copy(me).start()
        ix_copy(me).start()

    lane = lax.broadcasted_iota(jnp.int32, (8, 128), 1)
    sub = lax.broadcasted_iota(jnp.int32, (8, 128), 0)

    def pack(acc, value, k):
        return jnp.where((lane == k) | (lane == k - 1), pltpu.roll(value, k, 1), acc)

    def key(l, v):
        return 2 * (4 * l + v) + 1

    def halo_copies(s):
        low = rc(ef.at[s], ru.at[s], h_s.at[s, 0], h_r.at[s, 0], {"tm": me - step})
        up = rc(el.at[s], rl.at[s], h_s.at[s, 1], h_r.at[s, 1], {"tm": me + step})
        jl = rc(cs.at[s], cu.at[s], h_s.at[s, 2], h_r.at[s, 2], {"block": lower_b})
        ju = rc(cs.at[s], cl.at[s], h_s.at[s, 3], h_r.at[s, 3], {"block": upper_b})
        return low, up, jl, ju

    def face_copy(s, h, edge):
        return rc(edge.at[s], face.at[s, place], f_s.at[s, h], f_r.at[s, place], {"block": other0 + h})

    def face_wait(s, h):
        return rc(ef.at[s], face.at[s, h], f_s.at[s, h], f_r.at[s, h], {"block": other0 + h})

    def send_halos(s):
        low, up, jl, ju = halo_copies(s)

        @pl.when(is_last & (side == 0))
        def _():
            for h in range(half):
                face_copy(s, h, el).start()

        @pl.when(is_last & (side == 1))
        def _():
            for h in range(half):
                face_copy(s, h, ef).start()

        @pl.when(has_lower)
        def _():
            low.start()

        @pl.when(has_upper)
        def _():
            up.start()

        jl.start()
        ju.start()

    def take_level(l, accs):
        accs = list(accs)
        for v in range(4):
            for a in range(tiles):
                value = x0[l, v, pl.ds(8 * a, 8)]
                qa[l, v, pl.ds(PAD + 8 * a, 8)] = value
                accs[a] = pack(accs[a], value, key(l, v))
                if a == 0:
                    ef[0, pl.ds(4 * l + v, 1)] = value[0:1]
                if a == tiles - 1:
                    el[0, pl.ds(4 * l + v, 1)] = value[7:8]
        return tuple(accs)

    own.wait()
    accs = tuple(jnp.zeros((8, 128), jnp.float32) for _ in range(tiles))
    accs = lax.fori_loop(0, L, lambda j, c: take_level(me * L + j, c), accs)

    def arrive(t, c):
        p = peer(t)
        in_copy(p, p).wait_recv()
        return lax.fori_loop(0, L, lambda j, d: take_level(p * L + j, d), c)

    accs = lax.fori_loop(1, tm_n, arrive, accs)
    for a in range(tiles):
        cs[0, pl.ds(8 * a, 8)] = accs[a]
    send_halos(0)

    @pl.when(is_far)
    def _():
        own_far.wait()

        @pl.loop(1, tm_n)
        def _(p):
            far_copy(p).wait_recv()

        @pl.loop(0, NT)
        def _(l):
            for v in range(4):
                row = ff[l, pl.ds(v, 1)]
                qa[l, v, pl.ds(far_row, 1)] = row
                qb[l, v, pl.ds(far_row, 1)] = row

    @pl.when(is_last)
    def _():
        own_wt.wait()
        own_ix.wait()

        @pl.loop(0, tm_n - 1)
        def _(p):
            wt_copy(p).wait_recv()
            ix_copy(p).wait_recv()

        @pl.loop(0, NT // 2)
        def _(m):
            def ix(l):
                return jnp.broadcast_to(fi[lax.div(l, L), pl.ds(lax.rem(l, L), 1)], (8, 128))

            def wt(l, k):
                return jnp.broadcast_to(wts[l, pl.ds(k, 1)], (8, 128))

            start = jnp.where(sub < 4, ix(2 * m), ix(2 * m + 1))
            at = pl.ds(8 * m, 8)
            for k in range(K):
                src = start + k
                src = jnp.where(src >= cycle, src - cycle, src)
                lane_ix[k, at] = jnp.bitwise_and(src, 127)
                blk_ix[k, at] = lax.shift_right_logical(src, 7)
                ww[k, at] = jnp.where(sub < 4, wt(2 * m, k), wt(2 * m + 1, k))

    even, odd = split_coefficients(NT)
    speed_u = jnp.where(side == 0, mf[0, 0], mf[1, 0])
    speed_v = jnp.where(side == 0, mf[0, 1], mf[1, 1])
    odd_lane = jnp.bitwise_and(lane, 1) == 1
    edge_lane = {0: lane == 0, 127: lane == 127}

    def install(dst, src, at):
        @pl.loop(0, NT)
        def _(l):
            for v in range(4):
                dst[l, v, pl.ds(at, 1)] = src[pl.ds(4 * l + v, 1)]

    def out_copy(q, p, src_tm):
        return rc(q.at[lev(p), :, pl.ds(PAD, R)], out.at[:, :, rows(src_tm)],
                  out_s.at[p], out_r.at[src_tm], {"tm": p})

    for s, factor in enumerate(SECTION_FACTORS):
        q, nq = (qa, qb) if s % 2 == 0 else (qb, qa)
        final = s == nsec - 1

        @pl.loop(0, 4)
        def _(v):
            @pl.loop(0, tiles)
            def _(a):
                at = pl.ds(pl.multiple_of(PAD + 8 * a, 8), 8)
                terms = time_term([q[l, v, at] for l in range(NT)], even, odd)
                for l in range(NT):
                    nq[l, v, at] = terms[l]

        low, up, jl, ju = halo_copies(s)

        @pl.when(has_lower)
        def _():
            up.wait_recv()
            install(q, rl.at[s], PAD - 1)

        @pl.when(has_upper)
        def _():
            low.wait_recv()
            install(q, ru.at[s], PAD + R)

        jl.wait_recv()
        ju.wait_recv()

        @pl.when(is_last)
        def _():
            for h in range(half):
                face_wait(s, h).wait_recv()

            @pl.loop(0, NT // 2)
            def _(m):
                at = pl.ds(8 * m, 8)
                total = jnp.zeros((8, 128), jnp.float32)
                for k in range(K):
                    picked = jnp.zeros((8, 128), jnp.float32)
                    for h in range(half):
                        got = jnp.take_along_axis(face[s, h, at], lane_ix[k, at], axis=1)
                        picked = jnp.where(blk_ix[k, at] == h, got, picked)
                    total = total + ww[k, at] * picked
                gh[at] = total

            install(q, gh, ghost_row)

        mixed = []
        for a in range(tiles):
            at = pl.ds(8 * a, 8)
            mixed.append(jnp.where(odd_lane, pltpu.roll(cl[s, at], 1, 1), pltpu.roll(cu[s, at], 127, 1)))

        def level(l, accs):
            accs = list(accs)
            for a in range(tiles):
                base = PAD + 8 * a
                di, dj, lap = [], [], []
                for v in range(4):
                    x = q[l, v, pl.ds(base, 8)]
                    upx = q[l, v, pl.ds(base + 1, 8)]
                    dnx = q[l, v, pl.ds(base - 1, 8)]
                    border = pltpu.roll(mixed[a], 128 - key(l, v), 1)
                    left = jnp.where(edge_lane[0], border, pltpu.roll(x, 1, 1))
                    right = jnp.where(edge_lane[127], border, pltpu.roll(x, 127, 1))
                    di.append(upx - dnx)
                    dj.append(right - left)
                    lap.append(DISSIPATION * ((upx + dnx) + (right + left) - 4.0 * x))
                flux = [
                    speed_u * di[0] + di[1] + (speed_v * dj[0] + dj[2]),
                    speed_u * di[1] + di[3] + speed_v * dj[1],
                    speed_u * di[2] + (speed_v * dj[2] + dj[3]),
                    speed_u * di[3] + di[1] + (speed_v * dj[3] + dj[2]),
                ]
                for v in range(4):
                    term = nq[l, v, pl.ds(base, 8)]
                    new = x0[l, v, pl.ds(8 * a, 8)] - factor * (0.5 * flux[v] - lap[v] + term)
                    nq[l, v, pl.ds(base, 8)] = new
                    if not final:
                        accs[a] = pack(accs[a], new, key(l, v))
                        if a == 0:
                            ef[s + 1, pl.ds(4 * l + v, 1)] = new[0:1]
                        if a == tiles - 1:
                            el[s + 1, pl.ds(4 * l + v, 1)] = new[7:8]
            return tuple(accs)

        if not final:
            accs = tuple(jnp.zeros((8, 128), jnp.float32) for _ in range(tiles))
            accs = lax.fori_loop(0, NT, level, accs)
            for a in range(tiles):
                cs[s + 1, pl.ds(8 * a, 8)] = accs[a]
            send_halos(s + 1)
        else:
            def finish(t, c):
                p = peer(t)
                lax.fori_loop(0, L, lambda j, d: (level(p * L + j, ()), d)[1], 0)

                @pl.when(t < tm_n)
                def _():
                    out_copy(nq, p, me).start()

                return c

            lax.fori_loop(1, tm_n + 1, finish, 0)
            own_out = pltpu.make_async_copy(nq.at[lev(me), :, pl.ds(PAD, R)], out.at[:, :, rows(me)], loc.at[4])
            own_out.start()

            @pl.loop(1, tm_n)
            def _(t):
                p = peer(t)
                out_copy(nq, p, p).wait_recv()

            own_out.wait()

            @pl.loop(1, tm_n)
            def _(t):
                p = peer(t)
                out_copy(nq, p, me).wait_send()

    @pl.loop(1, tm_n)
    def _(t):
        p = peer(t)
        in_copy(p, me).wait_send()

    @pl.when(jnp.logical_not(is_far))
    def _():
        far_copy(me).wait_send()

    @pl.when(jnp.logical_not(is_last))
    def _():
        wt_copy(me).wait_send()
        ix_copy(me).wait_send()

    for s in range(nsec):
        low, up, jl, ju = halo_copies(s)

        @pl.when(has_lower)
        def _():
            low.wait_send()

        @pl.when(has_upper)
        def _():
            up.wait_send()

        jl.wait_send()
        ju.wait_send()

        @pl.when(is_last)
        def _():
            for h in range(half):
                face_wait(s, h).wait_send()


def shards(dims, state, far_field, face_index, face_weight, mean_flow):
    tm_n, half = dims
    L, _, rows, width = state.shape
    K = face_weight.shape[1]
    R = rows // tm_n
    NT = L * tm_n
    assert width == 128 and NT % 4 == 0 and R % 8 == 0 and 8 * NT <= width
    n = len(SECTION_FACTORS)
    f32 = jnp.float32
    hbm = pl.BlockSpec(memory_space=pl.ANY)
    dma = pltpu.SemaphoreType.DMA
    V = pltpu.VMEM
    return pl.pallas_call(
        functools.partial(kernel, (tm_n, half, L, R, K)),
        out_shape=jax.ShapeDtypeStruct(state.shape, f32),
        in_specs=[hbm, hbm, hbm, hbm, pl.BlockSpec(memory_space=pltpu.SMEM)],
        out_specs=hbm,
        scratch_shapes=[
            V((NT, 4, R, width), f32),
            V((NT, 4, R + 2 * PAD, width), f32),
            V((NT, 4, R + 2 * PAD, width), f32),
            V((n, 4 * NT, width), f32),
            V((n, 4 * NT, width), f32),
            V((n, 4 * NT, width), f32),
            V((n, 4 * NT, width), f32),
            V((n, R, width), f32),
            V((n, R, width), f32),
            V((n, R, width), f32),
            V((n, half, 4 * NT, width), f32),
            V((NT, 4, width), f32),
            V((NT, K, width), f32),
            V((tm_n, L, width), jnp.int32),
            V((K, 4 * NT, width), jnp.int32),
            V((K, 4 * NT, width), jnp.int32),
            V((K, 4 * NT, width), f32),
            V((4 * NT, width), f32),
            dma((tm_n,)), dma((tm_n,)), dma((tm_n,)), dma((tm_n,)),
            dma((3,)), dma((3, tm_n)),
            dma((n, 4)), dma((n, 4)),
            dma((n, half)), dma((n, half)),
            dma((5,)),
        ],
        compiler_params=pltpu.CompilerParams(
            collective_id=0, has_side_effects=True, vmem_limit_bytes=40 * 1024 * 1024),
    )(state, far_field, face_index, face_weight, mean_flow)


def solution(mesh):
    dims = (mesh.shape["tm"], mesh.shape["block"] // 2)
    in_specs = (
        P("tm", None, None, "block"),
        P("tm", None, "block"),
        P("tm", "block"),
        P("tm", None, "block"),
        P(),
    )
    out_specs = P("tm", None, None, "block")
    return jax.shard_map(functools.partial(shards, dims), mesh=mesh, in_specs=in_specs,
                         out_specs=out_specs, check_vma=False)
```

time: 572 us -> 88.8 us (0.16)
  the two profiles are of different devices: /device:TPU:0 before, /device:TPU:9 now
where the time goes in v1:
time: 88.8 us; the launch traced here: 88.6 us
  Pallas kernels  83.6 us (94%)
  local copies, waits for them, and re-layouts  4.93 us (6%)
    pallas_call x1, Pallas kernels, shards(): pl.pallas_call(functools.partial(kernel, (tm_n, half, L, R, K)), out_shap...  83.6 us
    unnamed x11, local copies, waits for them, and re-layouts  4.93 us

profile of v1, /device:TPU:9, one launch (start us, length us, event | category | flops | bytes accessed | tf_op | source)
XLA Modules:
  0.0 88.6 jit_solution(17419826496399425255)
XLA Ops:
  0.0 0.0 copy-start
  0.0 1.2 %copy-done = f32[2,4,256,128]{3,2,1,0:T(8,128)S(1)} copy-done((f32[2,4,256,128]{3,2,1,0:T(8,128)S(1)}, f32[2,4,256,128]{3,2,1,0:T(8,128)}, u32[]{:S(2)}) %copy-start) | copy-done | bytes 1048600
  1.2 0.0 copy-start.1
  1.2 0.7 copy-done.1
  1.9 0.0 copy-start.2
  1.9 0.7 copy-done.2
  2.6 0.0 copy-start.3
  2.6 0.7 copy-done.3
  3.3 0.0 copy-start.4
  3.3 0.7 copy-done.4
  4.0 83.6 %shard_map.55 = f32[2,4,256,128]{3,2,1,0:T(8,128)S(1)} custom-call(f32[2,4,256,128]{3,2,1,0:T(8,128)S(1)} %copy-done, f32[2,4,128]{2,1,0:T(4,128)S(1)} %copy-done.1, s32[2,128]{1,0:T(2,128)S(1)} %copy-done.3, f32[2,4,128]{2,1,0:T(4,128)S(1)} %copy-done.2, f32[2,2]{1,0:T(2,128)S(1)} %copy-done.4), custom_call_target="tpu_custom_call" | custom-call | tf_op jit(solution)/shard_map/pallas_call | solution.py:444
  87.6 1.0 %copy.7 = f32[2,4,256,128]{3,2,1,0:T(8,128)} copy(f32[2,4,256,128]{3,2,1,0:T(8,128)S(1)} %shard_map.55) | data formatting | bytes 2097152
Async XLA Ops:
  0.0 1.2 %copy-start = (f32[2,4,256,128]{3,2,1,0:T(8,128)S(1)}, f32[2,4,256,128]{3,2,1,0:T(8,128)}, u32[]{:S(2)}) copy-start(f32[2,4,256,128]{3,2,1,0:T(8,128)} %state.1) | copy-start | bytes 3145732
  1.2 0.7 copy-start.1
  1.9 0.7 copy-start.2
  2.6 0.7 copy-start.3
  3.3 0.7 copy-start.4

commit v2 on v1

--- a/solution.py
+++ b/solution.py
@@ -15,11 +15,11 @@
 MESH = pl.DeviceIdType.MESH
 
 
-def split_coefficients(count):
+def split_coefficients(count, scale):
     half = count // 2
     d = [0.0] + [0.5 * (-1) ** k / math.tan(math.pi * k / count) for k in range(1, half)] + [0.0]
-    even = [0.5 * OMEGA * (d[m] - d[half - m]) for m in range(half)]
-    odd = [0.5 * OMEGA * (d[m] + d[half - m]) for m in range(half)]
+    even = [0.5 * scale * (d[m] - d[half - m]) for m in range(half)]
+    odd = [0.5 * scale * (d[m] + d[half - m]) for m in range(half)]
     even[0] = odd[0] = 0.0
     return even, odd
 
@@ -87,11 +87,11 @@
         return pl.ds(p * L, L)
 
     def peer(t):
-        return lax.rem(me + t, tm_n)
+        return lax.rem(me + 1 + t, tm_n)
 
     bar = pltpu.get_barrier_semaphore()
 
-    @pl.loop(1, tm_n)
+    @pl.loop(0, tm_n - 1)
     def _(t):
         pl.semaphore_signal(bar, inc=1, device_id={"tm": peer(t)}, device_id_type=MESH)
 
@@ -110,7 +110,7 @@
     def in_copy(p, src_tm):
         return rc(state.at[:, :, rows(p)], x0.at[lev(src_tm)], in_s.at[p], in_r.at[src_tm], {"tm": p})
 
-    @pl.loop(1, tm_n)
+    @pl.loop(0, tm_n - 1)
     def _(t):
         p = peer(t)
         in_copy(p, me).start()
@@ -147,10 +147,11 @@
         ix_copy(me).start()
 
     lane = lax.broadcasted_iota(jnp.int32, (8, 128), 1)
+    lane_pair = jnp.bitwise_or(lane, 1)
     sub = lax.broadcasted_iota(jnp.int32, (8, 128), 0)
 
     def pack(acc, value, k):
-        return jnp.where((lane == k) | (lane == k - 1), pltpu.roll(value, k, 1), acc)
+        return jnp.where(lane_pair == k, pltpu.roll(value, k, 1), acc)
 
     def key(l, v):
         return 2 * (4 * l + v) + 1
@@ -210,11 +211,11 @@
     accs = lax.fori_loop(0, L, lambda j, c: take_level(me * L + j, c), accs)
 
     def arrive(t, c):
-        p = peer(t)
+        p = peer(tm_n - 2 - t)
         in_copy(p, p).wait_recv()
         return lax.fori_loop(0, L, lambda j, d: take_level(p * L + j, d), c)
 
-    accs = lax.fori_loop(1, tm_n, arrive, accs)
+    accs = lax.fori_loop(0, tm_n - 1, arrive, accs)
     for a in range(tiles):
         cs[0, pl.ds(8 * a, 8)] = accs[a]
     send_halos(0)
@@ -261,7 +262,6 @@
                 blk_ix[k, at] = lax.shift_right_logical(src, 7)
                 ww[k, at] = jnp.where(sub < 4, wt(2 * m, k), wt(2 * m + 1, k))
 
-    even, odd = split_coefficients(NT)
     speed_u = jnp.where(side == 0, mf[0, 0], mf[1, 0])
     speed_v = jnp.where(side == 0, mf[0, 1], mf[1, 1])
     odd_lane = jnp.bitwise_and(lane, 1) == 1
@@ -280,17 +280,78 @@
     for s, factor in enumerate(SECTION_FACTORS):
         q, nq = (qa, qb) if s % 2 == 0 else (qb, qa)
         final = s == nsec - 1
+        even, odd = split_coefficients(NT, OMEGA * factor)
+        hu, hv, hh = (0.5 * factor) * speed_u, (0.5 * factor) * speed_v, 0.5 * factor
 
         @pl.loop(0, 4)
         def _(v):
             @pl.loop(0, tiles)
             def _(a):
                 at = pl.ds(pl.multiple_of(PAD + 8 * a, 8), 8)
-                terms = time_term([q[l, v, at] for l in range(NT)], even, odd)
+                xs = [q[l, v, at] for l in range(NT)]
+                terms = time_term(xs, even, odd)
                 for l in range(NT):
-                    nq[l, v, at] = terms[l]
+                    first = x0[l, v, pl.ds(pl.multiple_of(8 * a, 8), 8)]
+                    nq[l, v, at] = first - (terms[l] + (4.0 * DISSIPATION * factor) * xs[l])
 
         low, up, jl, ju = halo_copies(s)
+        jl.wait_recv()
+        ju.wait_recv()
+        mixed = []
+        for a in range(tiles):
+            at = pl.ds(8 * a, 8)
+            mixed.append(jnp.where(odd_lane, pltpu.roll(cl[s, at], 1, 1), pltpu.roll(cu[s, at], 127, 1)))
+
+        def level(l, accs, which):
+            accs = list(accs)
+            for slot, a in enumerate(which):
+                base = PAD + 8 * a
+                di, dj, near = [], [], []
+                for v in range(4):
+                    x = q[l, v, pl.ds(base, 8)]
+                    upx = q[l, v, pl.ds(base + 1, 8)]
+                    dnx = q[l, v, pl.ds(base - 1, 8)]
+                    border = pltpu.roll(mixed[a], 128 - key(l, v), 1)
+                    left = jnp.where(edge_lane[0], border, pltpu.roll(x, 1, 1))
+                    right = jnp.where(edge_lane[127], border, pltpu.roll(x, 127, 1))
+                    di.append(upx - dnx)
+                    dj.append(right - left)
+                    near.append((DISSIPATION * factor) * ((upx + dnx) + (right + left)))
+                flux = [
+                    hu * di[0] + hv * dj[0] + hh * (di[1] + dj[2]),
+                    hu * di[1] + hv * dj[1] + hh * di[3],
+                    hu * di[2] + hv * dj[2] + hh * dj[3],
+                    hu * di[3] + hv * dj[3] + hh * (di[1] + dj[2]),
+                ]
+                for v in range(4):
+                    new = nq[l, v, pl.ds(base, 8)] + (near[v] - flux[v])
+                    nq[l, v, pl.ds(base, 8)] = new
+                    if not final:
+                        accs[slot] = pack(accs[slot], new, key(l, v))
+                        if a == 0:
+                            ef[s + 1, pl.ds(4 * l + v, 1)] = new[0:1]
+                        if a == tiles - 1:
+                            el[s + 1, pl.ds(4 * l + v, 1)] = new[7:8]
+            return tuple(accs)
+
+        def sweep(which):
+            zero = tuple(jnp.zeros((8, 128), jnp.float32) for _ in which)
+            step_by = 4 if NT % 4 == 0 else 1
+
+            def several(g, c):
+                for j in range(step_by):
+                    c = level(step_by * g + j, c, which)
+                return c
+
+            accs = lax.fori_loop(0, NT // step_by, several, zero)
+            if not final:
+                for slot, a in enumerate(which):
+                    cs[s + 1, pl.ds(8 * a, 8)] = accs[slot]
+
+        inner = tuple(range(1, tiles - 1))
+        outer = tuple(sorted({0, tiles - 1}))
+        if inner:
+            sweep(inner)
 
         @pl.when(has_lower)
         def _():
@@ -301,9 +362,6 @@
         def _():
             low.wait_recv()
             install(q, ru.at[s], PAD + R)
-
-        jl.wait_recv()
-        ju.wait_recv()
 
         @pl.when(is_last)
         def _():
@@ -324,78 +382,38 @@
 
             install(q, gh, ghost_row)
 
-        mixed = []
-        for a in range(tiles):
-            at = pl.ds(8 * a, 8)
-            mixed.append(jnp.where(odd_lane, pltpu.roll(cl[s, at], 1, 1), pltpu.roll(cu[s, at], 127, 1)))
-
-        def level(l, accs):
-            accs = list(accs)
-            for a in range(tiles):
-                base = PAD + 8 * a
-                di, dj, lap = [], [], []
-                for v in range(4):
-                    x = q[l, v, pl.ds(base, 8)]
-                    upx = q[l, v, pl.ds(base + 1, 8)]
-                    dnx = q[l, v, pl.ds(base - 1, 8)]
-                    border = pltpu.roll(mixed[a], 128 - key(l, v), 1)
-                    left = jnp.where(edge_lane[0], border, pltpu.roll(x, 1, 1))
-                    right = jnp.where(edge_lane[127], border, pltpu.roll(x, 127, 1))
-                    di.append(upx - dnx)
-                    dj.append(right - left)
-                    lap.append(DISSIPATION * ((upx + dnx) + (right + left) - 4.0 * x))
-                flux = [
-                    speed_u * di[0] + di[1] + (speed_v * dj[0] + dj[2]),
-                    speed_u * di[1] + di[3] + speed_v * dj[1],
-                    speed_u * di[2] + (speed_v * dj[2] + dj[3]),
-                    speed_u * di[3] + di[1] + (speed_v * dj[3] + dj[2]),
-                ]
-                for v in range(4):
-                    term = nq[l, v, pl.ds(base, 8)]
-                    new = x0[l, v, pl.ds(8 * a, 8)] - factor * (0.5 * flux[v] - lap[v] + term)
-                    nq[l, v, pl.ds(base, 8)] = new
-                    if not final:
-                        accs[a] = pack(accs[a], new, key(l, v))
-                        if a == 0:
-                            ef[s + 1, pl.ds(4 * l + v, 1)] = new[0:1]
-                        if a == tiles - 1:
-                            el[s + 1, pl.ds(4 * l + v, 1)] = new[7:8]
-            return tuple(accs)
-
         if not final:
-            accs = tuple(jnp.zeros((8, 128), jnp.float32) for _ in range(tiles))
-            accs = lax.fori_loop(0, NT, level, accs)
-            for a in range(tiles):
-                cs[s + 1, pl.ds(8 * a, 8)] = accs[a]
+            sweep(outer)
             send_halos(s + 1)
         else:
             def finish(t, c):
                 p = peer(t)
-                lax.fori_loop(0, L, lambda j, d: (level(p * L + j, ()), d)[1], 0)
-
-                @pl.when(t < tm_n)
+                for j in range(L):
+                    level(p * L + j, (None,) * len(outer), outer)
+
+                @pl.when(t < tm_n - 1)
                 def _():
                     out_copy(nq, p, me).start()
 
                 return c
 
-            lax.fori_loop(1, tm_n + 1, finish, 0)
+            lax.fori_loop(0, tm_n, finish, 0)
             own_out = pltpu.make_async_copy(nq.at[lev(me), :, pl.ds(PAD, R)], out.at[:, :, rows(me)], loc.at[4])
             own_out.start()
 
-            @pl.loop(1, tm_n)
+            @pl.loop(0, tm_n - 1)
             def _(t):
                 p = peer(t)
                 out_copy(nq, p, p).wait_recv()
 
             own_out.wait()
 
-            @pl.loop(1, tm_n)
+            @pl.loop(0, tm_n - 1)
             def _(t):
                 p = peer(t)
                 out_copy(nq, p, me).wait_send()
 
-    @pl.loop(1, tm_n)
+    @pl.loop(0, tm_n - 1)
     def _(t):
         p = peer(t)
         in_copy(p, me).wait_send()

time: 88.8 us -> 82.9 us (0.934)
  Pallas kernels: 83.6 us -> 77.6 us
    pallas_call x1, Pallas kernels: 83.6 us -> 77.6 us  [shards(): pl.pallas_call(functools.partial(kernel, (tm_n, half, L, R, K)), out_shap...]
where the time goes in v2:
time: 82.9 us; the launch traced here: 82.6 us
  Pallas kernels  77.6 us (94%)
  local copies, waits for them, and re-layouts  4.93 us (6%)
    pallas_call x1, Pallas kernels, shards(): pl.pallas_call(functools.partial(kernel, (tm_n, half, L, R, K)), out_shap...  77.6 us
    unnamed x11, local copies, waits for them, and re-layouts  4.93 us

profile of v2, /device:TPU:9, one launch (start us, length us, event | category | flops | bytes accessed | tf_op | source)
XLA Modules:
  0.0 82.6 jit_solution(5220681594467130341)
XLA Ops:
  0.0 0.0 copy-start
  0.0 1.2 %copy-done = f32[2,4,256,128]{3,2,1,0:T(8,128)S(1)} copy-done((f32[2,4,256,128]{3,2,1,0:T(8,128)S(1)}, f32[2,4,256,128]{3,2,1,0:T(8,128)}, u32[]{:S(2)}) %copy-start) | copy-done | bytes 1048600
  1.2 0.0 copy-start.1
  1.2 0.7 copy-done.1
  1.9 0.0 copy-start.2
  1.9 0.7 copy-done.2
  2.6 0.0 copy-start.3
  2.6 0.7 copy-done.3
  3.3 0.0 copy-start.4
  3.3 0.7 copy-done.4
  4.0 77.6 %shard_map.55 = f32[2,4,256,128]{3,2,1,0:T(8,128)S(1)} custom-call(f32[2,4,256,128]{3,2,1,0:T(8,128)S(1)} %copy-done, f32[2,4,128]{2,1,0:T(4,128)S(1)} %copy-done.1, s32[2,128]{1,0:T(2,128)S(1)} %copy-done.3, f32[2,4,128]{2,1,0:T(4,128)S(1)} %copy-done.2, f32[2,2]{1,0:T(2,128)S(1)} %copy-done.4), custom_call_target="tpu_custom_call" | custom-call | tf_op jit(solution)/shard_map/pallas_call | solution.py:462
  81.6 1.0 %copy.7 = f32[2,4,256,128]{3,2,1,0:T(8,128)} copy(f32[2,4,256,128]{3,2,1,0:T(8,128)S(1)} %shard_map.55) | data formatting | bytes 2097152
Async XLA Ops:
  0.0 1.2 %copy-start = (f32[2,4,256,128]{3,2,1,0:T(8,128)S(1)}, f32[2,4,256,128]{3,2,1,0:T(8,128)}, u32[]{:S(2)}) copy-start(f32[2,4,256,128]{3,2,1,0:T(8,128)} %state.1) | copy-start | bytes 3145732
  1.2 0.7 copy-start.1
  1.9 0.7 copy-start.2
  2.6 0.7 copy-start.3
  3.3 0.7 copy-start.4
